TPU v7x, 512 devices: a whole 4x8x8 slice. The times are simulated.
512 devices in a mesh: seq: 8 (over z), mp: 16 (over y, core), dp: 4 (over x).
Axes of the slice: x: 4, y: 8, z: 8, core: 2. Of those that a mesh axis runs over, the one named last changes fastest.
Arguments:
- tokens: bfloat16 [65536, 2048], P(('dp', 'seq'), 'mp'), parts along dimension 0, may hold values from -6 to 6
- w_query: bfloat16 [2048, 2048], P(None, 'mp'), may hold values from -0.125 to 0.125
- w_key: bfloat16 [2048, 2048], P(None, 'mp'), may hold values from -0.125 to 0.125
- w_value: bfloat16 [2048, 2048], P(None, 'mp'), may hold values from -0.125 to 0.125
- w_gate: bfloat16 [2048, 2048], P(None, 'mp'), may hold values from -0.125 to 0.125
- decay_exponent: int32 [16], P('mp'), may hold values from 5 to 16
- forget: float32 [65536, 16], P(('dp', 'seq'), 'mp'), parts along dimension 0, may hold values from 0 to 0.69
- norm_gain: float32 [2048], replicated, may hold values from 0.1 to 1.9
Outputs:
- retained: bfloat16 [65536, 2048], P(('dp', 'seq', 'mp')), parts along dimension 0
There are 4 independent parts, one for each index of `dp`. A program takes and returns all parts, laid end to end along the dimension named above; an argument that names none is the same for every part. Nothing has to cross between parts.
All inputs are finite; a program needn't handle non-finite values.
Results may differ from a plain program's by a relative error of at most 0.015.
Values may be sent and summed in bfloat16 or wider, within the bound.
A program may use at most 64 MiB of HBM per device.

v0:
```python
import jax
import jax.numpy as jnp
from jax import lax
from jax.sharding import PartitionSpec as P

HEADS = 16
DH = 128


def from_everyone(shard, axis):
    copies = jnp.broadcast_to(shard, (lax.axis_size(axis), *shard.shape))
    return lax.all_to_all(copies, axis, split_axis=0, concat_axis=0, tiled=True)


def collected_together(shard, axis):
    leaves = jax.tree.leaves(shard)
    sequence = sorted(range(len(leaves)), key=lambda k: -leaves[k].size)
    width = (1, *leaves[sequence[0]].shape)[-1]
    lines = [
        jnp.pad(leaves[k].reshape(-1), (0, -leaves[k].size % width)).reshape(-1, width)
        for k in sequence
    ]
    both, at, found = (from_everyone(jnp.concatenate(lines), axis), 0, {})
    for k, line in zip(sequence, lines):
        section = both[:, at : at + len(line)].reshape(len(both), -1)
        found[k] = section[:, : leaves[k].size].reshape(-1, *leaves[k].shape)
        at += len(line)
    numbers = iter(range(len(leaves)))
    return jax.tree.map(lambda _: found[next(numbers)], shard)


def folded_in_pairs(pieces, combine):
    while len(jax.tree.leaves(pieces)[0]) > 1:
        pieces = jax.vmap(combine)(
            *(jax.tree.map(lambda part: part[side::2], pieces) for side in (0, 1))
        )
    return jax.tree.map(lambda part: part[0], pieces)


def prefix_2(shard, axis, combine, identity):
    size, index = (lax.axis_size(axis), lax.axis_index(axis))
    passed = jnp.arange(size) < index

    def kept(part, zero, own):
        part = jnp.where(
            passed.reshape(-1, *(1 for _ in own.shape)),
            part.astype(own.dtype),
            jnp.asarray(zero, own.dtype),
        )
        return part

    pieces = collected_together(
        jax.tree.map(lambda part, kind: part.astype(kind), shard, (jnp.bfloat16, jnp.bfloat16)),
        axis,
    )
    return folded_in_pairs(jax.tree.map(kept, pieces, identity, shard), combine)


def over_copies(shard, axis):
    return from_everyone(shard, axis).sum(axis=0)


def run_blocks(queries, key_rows, values, logdecay, head_count, head_width):
    seq_rows = queries.shape[0]
    block_rows = 512
    block_count = seq_rows // block_rows

    def shaped(source):
        return source.reshape(block_count, block_rows, head_count, head_width)

    decays = logdecay.reshape(block_count, block_rows, head_count)
    position = lax.broadcasted_iota(jnp.int32, (block_rows, block_rows), 0)
    earlier = lax.broadcasted_iota(jnp.int32, (block_rows, block_rows), 1)
    causal = position >= earlier

    def advance(carried, pieces):
        kv_state, offset = carried
        query_blk, key_blk, value_blk, decay_blk = pieces
        running = jnp.cumsum(decay_blk, axis=0)
        heads_first = running.T
        log_gap = heads_first[:, :, None] - heads_first[:, None, :]
        decay_mask = jnp.where(causal[None], jnp.exp(jnp.where(causal[None], log_gap, 0.0)), 0.0)
        scores = jnp.einsum("tha,sha->hts", query_blk, key_blk, preferred_element_type=jnp.float32)
        scores = (scores * decay_mask).astype(jnp.bfloat16)
        inner = jnp.einsum("hts,shb->thb", scores, value_blk, preferred_element_type=jnp.float32)
        query_float = query_blk.astype(jnp.float32)
        earlier_part = jnp.einsum(
            "tha,hab->thb", query_float * jnp.exp(running)[:, :, None], kv_state
        )
        query_device = query_float * jnp.exp(running + offset[None, :])[:, :, None]
        key_scaled = key_blk.astype(jnp.float32) * jnp.exp(running[-1:] - running)[:, :, None]
        kv_state = jnp.exp(running[-1])[:, None, None] * kv_state + jnp.einsum(
            "sha,shb->hab", key_scaled, value_blk.astype(jnp.float32)
        )
        return ((kv_state, offset + running[-1]), (inner + earlier_part, query_device))

    initial = (
        jnp.zeros((head_count, head_width, head_width), jnp.float32),
        jnp.zeros((head_count,), jnp.float32),
    )
    final, outputs = lax.scan(
        advance, initial, (shaped(queries), shaped(key_rows), shaped(values), decays)
    )
    local_part = outputs[0].reshape(seq_rows, head_count, head_width)
    query_device = outputs[1].reshape(seq_rows, head_count, head_width)
    return (local_part, query_device, final[0], final[1])


def combine_states(before, after):
    return (before[0] * after[0], after[0][:, None, None] * before[1] + after[1])


def body(tokens, w_query, w_key, w_value, w_gate, decay_exponent, forget, norm_gain):
    seq_rows = tokens.shape[0]
    local_width = w_query.shape[1]
    head_count = decay_exponent.shape[0]
    head_width = local_width // head_count
    empty = jnp.zeros((seq_rows, local_width), jnp.float32)
    summed = (empty, empty, empty, empty)
    piece = lax.all_gather(tokens, "mp", axis=1, tiled=True)
    results = []
    for weight, partial_value in zip((w_query, w_key, w_value, w_gate), summed):
        results.append(jnp.dot(piece, weight, preferred_element_type=jnp.float32))
    projected = tuple(results)
    queries = projected[0].astype(jnp.bfloat16)
    key_rows = (projected[1] * DH ** (-0.5)).astype(jnp.bfloat16)
    values = projected[2].astype(jnp.bfloat16)
    gate = projected[3].astype(jnp.bfloat16)
    rate = jnp.log1p(-jnp.exp2(-decay_exponent.astype(jnp.float32)))
    logdecay = rate[None, :] - forget
    local_part, query_device, own_state, own_total = run_blocks(
        queries, key_rows, values, logdecay, head_count, head_width
    )
    prefix = prefix_2(
        (jnp.exp(own_total), own_state),
        "seq",
        combine_states,
        (jnp.ones_like(own_total), jnp.zeros_like(own_state)),
    )
    incoming = prefix[1]
    from_before = jnp.einsum("tha,hab->thb", query_device, incoming)
    output = (local_part + from_before).astype(jnp.bfloat16).reshape(seq_rows, local_width)
    output_float = output.astype(jnp.float32)
    squares = over_copies(jnp.sum(output_float * output_float, axis=1), "mp")
    rstd = lax.rsqrt(squares / (HEADS * DH) + 1e-06)
    gain_here = lax.dynamic_slice_in_dim(
        norm_gain, lax.axis_index("mp") * local_width, local_width, 0
    )
    gated = (
        jax.nn.silu(gate.astype(jnp.float32)) * output_float * rstd[:, None] * gain_here[None, :]
    )
    return lax.all_to_all(gated.astype(jnp.bfloat16), "mp", split_axis=0, concat_axis=1, tiled=True)


def solution(mesh):
    placed = (
        P(("dp", "seq"), "mp"),
        P(None, "mp"),
        P(None, "mp"),
        P(None, "mp"),
        P(None, "mp"),
        P("mp"),
        P(("dp", "seq"), "mp"),
        P(),
    )
    return jax.shard_map(
        body, mesh=mesh, in_specs=placed, out_specs=P(("dp", "seq", "mp"), None), check_vma=False
    )
```

profile of v0, /device:TPU:1, one launch (start us, length us, event | category | flops | bytes accessed | tf_op | source)
XLA Modules:
  0.0 194.3 jit_solution(12837014939397995423)
XLA Ops:
  6.5 0.7 all-gather.2.cloned.1.call-update
  8.0 0.7 broadcast_subtract_fusion
  8.7 76.1 %all-gather.2.cloned.1.call-done = bf16[2048,2048]{1,0:T(8,128)(2,1)} async-done(((bf16[2048,128]{1,0:T(8,128)(2,1)}), bf16[2048,2048]{1,0:T(8,128)(2,1)}) %all-gather.2.cloned.1.call-update) | async-done | bytes 8388624 | tf_op jit(solution)/shard_map/all_gather | solution.py:120
  84.8 5.9 %fusion.52 = bf16[2048,128]{1,0:T(8,128)(2,1)S(1)} fusion(bf16[2048,2048]{1,0:T(8,128)(2,1)} %all-gather.2.cloned.1.call-done, bf16[2048,128]{1,0:T(8,128)(2,1)S(1)} %copy-done), kind=kOutput, calls=%fused_computation.61 | convolution fusion | flops 1074266112 | bytes 9437184 | tf_op jit(solution)/shard_map/dot_general | solution.py:123
  90.7 3.3 %convolution_convert_fusion.1 = bf16[2048,128]{1,0:T(8,128)(2,1)} fusion(bf16[2048,2048]{1,0:T(8,128)(2,1)S(1)} %copy-done.1, bf16[2048,128]{1,0:T(8,128)(2,1)S(1)} %copy-done.2), kind=kOutput, calls=%fused_computation.57 | convolution fusion | flops 1074003968 | bytes 9437184 | tf_op jit(solution)/shard_map/dot_general | solution.py:123
  94.0 2.4 %convolution_convert_fusion = bf16[2048,128]{1,0:T(8,128)(2,1)S(1)} fusion(bf16[2048,2048]{1,0:T(8,128)(2,1)S(1)} %copy-done.1, bf16[2048,128]{1,0:T(8,128)(2,1)S(1)} %copy-done.3), kind=kOutput, calls=%fused_computation.56 | convolution fusion | flops 1074003968 | bytes 9437184 | tf_op jit(solution)/shard_map/dot_general | solution.py:123
  96.4 29.3 %while.18 = (s32[]{:T(128)}, f32[1,128,128]{2,1,0:T(8,128)S(1)}, f32[1]{0:T(128)}, f32[4,512,1,128]{3,1,0,2:T(8,128)S(1)}, bf16[4,512,1,128]{3,1,2,0:T(8,128)(2,...) while((s32[]{:T(128)}, f32[1,128,128]{2,1,0:T(8,128)S(1)}, ...), condition=%wide.region_3.4_spmd.clone.clone, body=%wide.region_0.3_spmd.clone.clone.sunk | while | flops 169935888 | bytes 3247952 | solution.py:101
  97.8 0.6 slice.109
  99.9 1.5 fusion.91
  101.6 1.3 fusion.90
  102.9 0.8 fusion.92
  107.3 1.5 fusion.91
  108.9 1.3 fusion.90
  110.2 0.8 fusion.92
  114.6 1.5 fusion.91
  116.2 1.3 fusion.90
  117.5 0.8 fusion.92
  119.7 0.6 slice.109
  121.9 1.5 fusion.91
  123.5 1.3 fusion.90
  124.8 0.8 fusion.92
  125.7 0.8 broadcast_in_dim.45
  126.5 4.0 %all-to-all-start = ((bf16[8,129,128]{2,1,0:T(8,128)(2,1)}), bf16[8,129,128]{2,1,0:T(8,128)(2,1)S(1)}, u32[]{:S(2)}, u32[]{:S(2)}) async-start(bf16[8,129,128]{2,1,0:T(8,128)(2,1)} %broadcast_in_dim.45), calls=%async_computation | async-start | bytes 557056 | tf_op jit(solution)/shard_map/all_to_all | solution.py:12
  130.5 12.5 %all-to-all-done = bf16[8,129,128]{2,1,0:T(8,128)(2,1)S(1)} async-done(((bf16[8,129,128]{2,1,0:T(8,128)(2,1)}), bf16[8,129,128]{2,1,0:T(8,128)(2,1)S(1)}, u32[]{:S(2)}, u32[]{:S(2)}) %all-to-all-start) | async-done | bytes 264224 | tf_op jit(solution)/shard_map/all_to_all | solution.py:12
  144.2 2.1 %multiply_reduce_fusion = (f32[2048]{0:T(1024)S(1)}, f32[2048,128]{1,0:T(8,128)S(1)}) fusion(f32[2048,1,128]{2,0,1:T(8,128)S(1)} %bitcast.167, bf16[2048,128]{1,0:T(8,128)(2,1)} %bitcast.171, f32[2,1,128,128]{3,2,1,0:T(8,128)S(1)} %slice_add_fusion.1, f32[]{:T(128)} %bitcast.12), kind=kOutput, calls=%fused_computation.65 | convolution fusion | flops 68450304 | bytes 2760708 | tf_op jit(solution)/shard_map/tha,hab->thb/dot_general | solution.py:141
  146.3 0.7 broadcast_in_dim.49
  147.0 4.9 %all-to-all-start.1 = ((f32[16,1,2048]{2,1,0:T(1,128)}), f32[16,1,2048]{2,1,0:T(1,128)S(1)}, u32[]{:S(2)}, u32[]{:S(2)}) async-start(f32[16,1,2048]{2,1,0:T(1,128)} %broadcast_in_dim.49), calls=%async_computation.1 | async-start | bytes 262144 | tf_op jit(solution)/shard_map/all_to_all | solution.py:12
  151.9 0.8 dynamic_slice.17
  152.7 8.1 %all-to-all-done.1 = f32[16,1,2048]{2,1,0:T(1,128)S(1)} async-done(((f32[16,1,2048]{2,1,0:T(1,128)}), f32[16,1,2048]{2,1,0:T(1,128)S(1)}, u32[]{:S(2)}, u32[]{:S(2)}) %all-to-all-start.1) | async-done | bytes 131104 | tf_op jit(solution)/shard_map/all_to_all | solution.py:12
  160.9 5.8 %multiply_convert_fusion = bf16[2048,128]{1,0:T(8,128)(2,1)S(1)} fusion(f32[2048,128]{1,0:T(8,128)S(1)} %get-tuple-element.204, bf16[2048,2048]{1,0:T(8,128)(2,1)} %all-gather.2.cloned.1.call-done, bf16[2048,128]{1,0:T(8,128)(2,1)} %param.14, f32[128]{0:T(128)S(1)} %dynamic_slice.17, f32[2048]{0:T(1024)S(1)} %add_rsqrt_fusion), kind=kOutput, calls=%fused_computation.64 | convolution fusion | flops 1076363264 | bytes 10494464 | tf_op jit(solution)/shard_map/dot_general | solution.py:123
  166.7 19.9 %all_to_all.30 = bf16[16,128,128]{2,1,0:T(8,128)(2,1)S(1)} all-to-all(bf16[16,128,128]{2,1,0:T(8,128)(2,1)S(1)} %bitcast.170), channel_id=1, replica_groups=mesh['seq'=8,'mp'=16,'dp'=4] {'mp'}, dimensions={0} | all-to-all | bytes 1048576 | tf_op jit(solution)/shard_map/all_to_all | solution.py:152
  186.6 0.9 copy_bitcast_fusion
  (81 shorter events, 10.0 us)
Async XLA Ops:
  6.5 78.2 %copy-start = (bf16[2048,128]{1,0:T(8,128)(2,1)S(1)}, bf16[2048,128]{1,0:T(8,128)(2,1)}, u32[]{:S(2)}) copy-start(bf16[2048,128]{1,0:T(8,128)(2,1)} %param.12) | copy-start | bytes 1572868
  6.5 84.1 %copy-start.2 = (bf16[2048,128]{1,0:T(8,128)(2,1)S(1)}, bf16[2048,128]{1,0:T(8,128)(2,1)}, u32[]{:S(2)}) copy-start(bf16[2048,128]{1,0:T(8,128)(2,1)} %param.13) | copy-start | bytes 1572868
  6.5 78.2 %all-gather.2.cloned.1.call-start = ((), (), s32[]{:S(2)}) async-start(), calls=%async_computation.3 | async-start | bytes 8912896 | tf_op jit(solution)/shard_map/all_gather | solution.py:120
  84.8 5.9 %copy-start.1 = (bf16[2048,2048]{1,0:T(8,128)(2,1)S(1)}, bf16[2048,2048]{1,0:T(8,128)(2,1)}, u32[]{:S(2)}) copy-start(bf16[2048,2048]{1,0:T(8,128)(2,1)} %all-gather.2.cloned.1.call-done) | copy-start | bytes 25165828
  90.7 3.3 %copy-start.3 = (bf16[2048,128]{1,0:T(8,128)(2,1)S(1)}, bf16[2048,128]{1,0:T(8,128)(2,1)}, u32[]{:S(2)}) copy-start(bf16[2048,128]{1,0:T(8,128)(2,1)} %param.11) | copy-start | bytes 1572868
  126.5 16.6 %all-to-all-start = ((bf16[8,129,128]{2,1,0:T(8,128)(2,1)}), bf16[8,129,128]{2,1,0:T(8,128)(2,1)S(1)}, u32[]{:S(2)}, u32[]{:S(2)}) async-start(bf16[8,129,128]{2,1,0:T(8,128)(2,1)} %broadcast_in_dim.45), calls=%async_computation | async-start | bytes 557056 | tf_op jit(solution)/shard_map/all_to_all | solution.py:12
  147.0 13.8 %all-to-all-start.1 = ((f32[16,1,2048]{2,1,0:T(1,128)}), f32[16,1,2048]{2,1,0:T(1,128)S(1)}, u32[]{:S(2)}, u32[]{:S(2)}) async-start(f32[16,1,2048]{2,1,0:T(1,128)} %broadcast_in_dim.49), calls=%async_computation.1 | async-start | bytes 262144 | tf_op jit(solution)/shard_map/all_to_all | solution.py:12
Sparse Core Ops, SparseCore 0:
  9.4 75.3 all-gather.1
where the time goes:
time: 195 us; the launch traced here: 194 us
  waiting for transfers between devices  97.4 us (50%)
  matrix products  31.5 us (16%)
  blocking collectives  19.9 us (10%)
  between operations  14.3 us (7%)
  local copies, waits for them, and re-layouts  10.2 us (5%)
  starting transfers between devices  8.92 us (5%)
  other arithmetic  6.83 us (4%)
  loops' own time  5.24 us (3%)
    all_gather x1, waiting for transfers between devices, body(): piece = lax.all_gather(tokens, 'mp', axis=1, tiled=True)  76.1 us
    all_to_all x2, waiting for transfers between devices, from_everyone(): return lax.all_to_all(copies, axis, split_axis=0, concat_axis=0, tiled=True)  20.7 us
    all_to_all x1, blocking collectives, body(): lax.all_to_all(gated.astype(jnp.bfloat16), 'mp', split_axis=0, concat_axi...  19.9 us
    dot_general x4, matrix products, body(): results.append(jnp.dot(piece, weight, preferred_element_type=jnp.float32))  17.3 us
    all_to_all x2, starting transfers between devices, from_everyone(): return lax.all_to_all(copies, axis, split_axis=0, concat_axis=0, tiled=True)  8.92 us
    dot_general x4, matrix products, advance(): jnp.einsum('hts,shb->thb', scores, value_blk, preferred_element_type=jnp....  5.87 us
    another operation x1, loops' own time, run_blocks(): lax.scan(advance, initial, (shaped(queries), shaped(key_rows), shaped(val...  5.24 us
    dot_general x4, matrix products, advance(): jnp.einsum('sha,shb->hab', key_scaled, value_blk.astype(jnp.float32))  5.01 us
  transfers between devices with their start and end apart: 3, of which 3 were waited for; matrix products, arithmetic and copies ran while one was open for 1% of the time, Pallas kernels for 0%

commit v1 on v0

--- a/solution.py
+++ b/solution.py
@@ -117,7 +117,9 @@
     head_width = local_width // head_count
     empty = jnp.zeros((seq_rows, local_width), jnp.float32)
     summed = (empty, empty, empty, empty)
-    piece = lax.all_gather(tokens, "mp", axis=1, tiled=True)
+    piece = jnp.concatenate(
+        lax.all_to_all(jnp.stack([tokens] * lax.axis_size("mp")), "mp", 0, 0), axis=1
+    )
     results = []
     for weight, partial_value in zip((w_query, w_key, w_value, w_gate), summed):
         results.append(jnp.dot(piece, weight, preferred_element_type=jnp.float32))

time: 195 us -> 315 us (1.62)
  waiting for transfers between devices: 97.4 us -> 201 us
  starting transfers between devices: 8.92 us -> 26.4 us
  between operations: 14.3 us -> 0.99 us
  matrix products: 31.5 us -> 38.4 us
  local copies, waits for them, and re-layouts: 10.2 us -> 16 us
    all_to_all x0 -> x1, waiting for transfers between devices: none -> 183 us  [body(): lax.all_to_all(jnp.stack([tokens] * lax.axis_size('mp')), 'mp', 0, 0)]
    all_gather x1 -> x0, waiting for transfers between devices: 76.1 us -> none  [body(): piece = lax.all_gather(tokens, 'mp', axis=1, tiled=True)]
    all_to_all x0 -> x1, starting transfers between devices: none -> 11.4 us  [body(): lax.all_to_all(jnp.stack([tokens] * lax.axis_size('mp')), 'mp', 0, 0)]
    dot_general x4, matrix products: 17.3 us -> 24.3 us  [body(): results.append(jnp.dot(piece, weight, preferred_element_type=jnp.float32))]
    all_to_all x2, starting transfers between devices: 8.92 us -> 14.9 us  [from_everyone(): return lax.all_to_all(copies, axis, split_axis=0, concat_axis=0, tiled=True)]
    another operation x8 -> x9, local copies, waits for them, and re-layouts: 0.3 us -> 4.6 us  [the longest x1 4.3 us: body(): jnp.stack([tokens] * lax.axis_size('mp'))]
  transfers between devices with their start and end apart: 3 -> 3, of which waited for: 3 -> 3; matrix products, arithmetic and copies ran while one was open for 1% -> 0% of each run, Pallas kernels for 0% -> 0%
where the time goes in v1:
time: 315 us
  waiting for transfers between devices  201 us (64%)
  matrix products  38.4 us (12%)
  starting transfers between devices  26.4 us (8%)
  blocking collectives  19.9 us (6%)
  local copies, waits for them, and re-layouts  16 us (5%)
  other arithmetic  6.13 us (2%)
  loops' own time  5.47 us (2%)
    all_to_all x1, waiting for transfers between devices, body(): lax.all_to_all(jnp.stack([tokens] * lax.axis_size('mp')), 'mp', 0, 0)  183 us
    dot_general x4, matrix products, body(): results.append(jnp.dot(piece, weight, preferred_element_type=jnp.float32))  24.3 us
    all_to_all x1, blocking collectives, body(): lax.all_to_all(gated.astype(jnp.bfloat16), 'mp', split_axis=0, concat_axi...  19.9 us
    all_to_all x2, waiting for transfers between devices, from_everyone(): return lax.all_to_all(copies, axis, split_axis=0, concat_axis=0, tiled=True)  18.7 us
    all_to_all x2, starting transfers between devices, from_everyone(): return lax.all_to_all(copies, axis, split_axis=0, concat_axis=0, tiled=True)  14.9 us
    all_to_all x1, starting transfers between devices, body(): lax.all_to_all(jnp.stack([tokens] * lax.axis_size('mp')), 'mp', 0, 0)  11.4 us
  transfers between devices with their start and end apart: 3, of which 3 were waited for; matrix products, arithmetic and copies ran while one was open for 0% of the time, Pallas kernels for 0%

profile of v1, /device:TPU:1, one launch (start us, length us, event | category | flops | bytes accessed | tf_op | source)
XLA Modules:
  0.0 314.6 jit_solution(14915818654427561245)
XLA Ops:
  0.0 1.3 copy.56
  1.3 4.3 %stack.2 = bf16[16,2048,128]{1,2,0:T(8,128)(2,1)} broadcast(bf16[2048,128]{0,1:T(8,128)(2,1)S(1)} %copy.56), dimensions={1,2} | broadcast | bytes 8912896 | tf_op jit(solution)/shard_map/stack | solution.py:121
  5.6 11.4 %all-to-all-start = ((bf16[16,2048,128]{1,2,0:T(8,128)(2,1)}), bf16[16,2048,128]{1,2,0:T(8,128)(2,1)}, u32[]{:S(2)}, u32[]{:S(2)}) async-start(bf16[16,2048,128]{1,2,0:T(8,128)(2,1)} %stack.2), calls=%async_computation | async-start | bytes 16777216 | tf_op jit(solution)/shard_map/all_to_all | solution.py:121
  17.9 182.6 %all-to-all-done = bf16[16,2048,128]{1,2,0:T(8,128)(2,1)} async-done(((bf16[16,2048,128]{1,2,0:T(8,128)(2,1)}), bf16[16,2048,128]{1,2,0:T(8,128)(2,1)}, u32[]{:S(2)}, u32[]{:S(2)}) %all-to-all-start) | async-done | bytes 8388640 | tf_op jit(solution)/shard_map/all_to_all | solution.py:121
  200.5 5.8 %convolution_convert_fusion = bf16[2048,128]{1,0:T(8,128)(2,1)S(1)} fusion(bf16[2048,2048]{0,1:T(8,128)(2,1)} %bitcast.1, bf16[2048,128]{1,0:T(8,128)(2,1)S(1)} %copy-done), kind=kOutput, calls=%fused_computation.56 | convolution fusion | flops 1074003968 | bytes 9437184 | tf_op jit(solution)/shard_map/dot_general | solution.py:125
  206.3 5.8 %fusion.52 = bf16[2048,128]{1,0:T(8,128)(2,1)S(1)} fusion(bf16[2048,2048]{0,1:T(8,128)(2,1)} %bitcast.1, bf16[2048,128]{1,0:T(8,128)(2,1)S(1)} %copy-done.2), kind=kOutput, calls=%fused_computation.61 | convolution fusion | flops 1074266112 | bytes 9437184 | tf_op jit(solution)/shard_map/dot_general | solution.py:125
  212.2 6.6 %convolution_convert_fusion.1 = bf16[2048,128]{1,0:T(8,128)(2,1)} fusion(bf16[2048,2048]{0,1:T(8,128)(2,1)} %bitcast.1, bf16[2048,128]{1,0:T(8,128)(2,1)S(1)} %copy-done.3), kind=kOutput, calls=%fused_computation.57 | convolution fusion | flops 1074003968 | bytes 9437184 | tf_op jit(solution)/shard_map/dot_general | solution.py:125
  218.8 29.6 %while.18 = (s32[]{:T(128)}, f32[1,128,128]{2,1,0:T(8,128)S(1)}, f32[1]{0:T(128)}, f32[4,512,1,128]{3,1,0,2:T(8,128)S(1)}, bf16[4,512,1,128]{3,1,2,0:T(8,128)(2,...) while((s32[]{:T(128)}, f32[1,128,128]{2,1,0:T(8,128)S(1)}, ...), condition=%wide.region_3.4_spmd.clone.clone, body=%wide.region_0.3_spmd.clone.clone.sunk | while | flops 169935888 | bytes 3247952 | solution.py:101
  222.5 1.5 fusion.91
  224.2 1.3 fusion.90
  225.4 0.8 fusion.92
  227.7 0.6 slice.109
  229.9 1.5 fusion.91
  231.6 1.3 fusion.90
  232.8 0.8 fusion.92
  237.3 1.5 fusion.91
  239.0 1.3 fusion.90
  240.2 0.8 fusion.92
  244.7 1.5 fusion.91
  246.4 1.3 fusion.90
  247.6 0.8 fusion.92
  248.5 0.8 broadcast_in_dim.45
  249.3 7.3 %all-to-all-start.1 = ((bf16[8,129,128]{2,1,0:T(8,128)(2,1)}), bf16[8,129,128]{2,1,0:T(8,128)(2,1)S(1)}, u32[]{:S(2)}, u32[]{:S(2)}) async-start(bf16[8,129,128]{2,1,0:T(8,128)(2,1)} %broadcast_in_dim.45), calls=%async_computation.1 | async-start | bytes 557056 | tf_op jit(solution)/shard_map/all_to_all | solution.py:12
  256.6 10.6 %all-to-all-done.1 = bf16[8,129,128]{2,1,0:T(8,128)(2,1)S(1)} async-done(((bf16[8,129,128]{2,1,0:T(8,128)(2,1)}), bf16[8,129,128]{2,1,0:T(8,128)(2,1)S(1)}, u32[]{:S(2)}, u32[]{:S(2)}) %all-to-all-start.1) | async-done | bytes 264224 | tf_op jit(solution)/shard_map/all_to_all | solution.py:12
  268.3 2.1 multiply_reduce_fusion
  270.4 0.7 broadcast_in_dim.49
  271.1 7.7 %all-to-all-start.2 = ((f32[16,1,2048]{2,1,0:T(1,128)}), f32[16,1,2048]{2,1,0:T(1,128)S(1)}, u32[]{:S(2)}, u32[]{:S(2)}) async-start(f32[16,1,2048]{2,1,0:T(1,128)} %broadcast_in_dim.49), calls=%async_computation.2 | async-start | bytes 262144 | tf_op jit(solution)/shard_map/all_to_all | solution.py:12
  278.8 0.8 dynamic_slice.17
  279.6 8.1 %all-to-all-done.2 = f32[16,1,2048]{2,1,0:T(1,128)S(1)} async-done(((f32[16,1,2048]{2,1,0:T(1,128)}), f32[16,1,2048]{2,1,0:T(1,128)S(1)}, u32[]{:S(2)}, u32[]{:S(2)}) %all-to-all-start.2) | async-done | bytes 131104 | tf_op jit(solution)/shard_map/all_to_all | solution.py:12
  287.8 6.0 %multiply_convert_fusion = bf16[2048,128]{1,0:T(8,128)(2,1)S(1)} fusion(f32[2048,128]{1,0:T(8,128)S(1)} %get-tuple-element.204, bf16[2048,2048]{0,1:T(8,128)(2,1)} %bitcast.1, bf16[2048,128]{1,0:T(8,128)(2,1)} %param.14, f32[128]{0:T(128)S(1)} %dynamic_slice.17, f32[2048]{0:T(1024)S(1)} %add_rsqrt_fusion), kind=kOutput, calls=%fused_computation.64 | convolution fusion | flops 1076363264 | bytes 10494464 | tf_op jit(solution)/shard_map/dot_general | solution.py:125
  293.8 19.9 %all_to_all.35 = bf16[16,128,128]{2,1,0:T(8,128)(2,1)S(1)} all-to-all(bf16[16,128,128]{2,1,0:T(8,128)(2,1)S(1)} %bitcast.173), channel_id=1, replica_groups=mesh['seq'=8,'mp'=16,'dp'=4] {'mp'}, dimensions={0} | all-to-all | bytes 1048576 | tf_op jit(solution)/shard_map/all_to_all | solution.py:154
  313.7 0.9 copy_bitcast_fusion
  (82 shorter events, 10.8 us)
Async XLA Ops:
  0.0 200.5 %copy-start = (bf16[2048,128]{1,0:T(8,128)(2,1)S(1)}, bf16[2048,128]{1,0:T(8,128)(2,1)}, u32[]{:S(2)}) copy-start(bf16[2048,128]{1,0:T(8,128)(2,1)} %param.11) | copy-start | bytes 1572868
  5.6 12.3 %copy-start.1 = (f32[2048,1]{0,1:T(1,128)S(1)}, f32[2048,1]{0,1:T(1,128)}, u32[]{:S(2)}) copy-start(f32[2048,1]{0,1:T(1,128)} %param.16) | copy-start | bytes 24580
  5.6 194.9 %all-to-all-start = ((bf16[16,2048,128]{1,2,0:T(8,128)(2,1)}), bf16[16,2048,128]{1,2,0:T(8,128)(2,1)}, u32[]{:S(2)}, u32[]{:S(2)}) async-start(bf16[16,2048,128]{1,2,0:T(8,128)(2,1)} %stack.2), calls=%async_computation | async-start | bytes 16777216 | tf_op jit(solution)/shard_map/all_to_all | solution.py:121
  17.1 189.2 %copy-start.2 = (bf16[2048,128]{1,0:T(8,128)(2,1)S(1)}, bf16[2048,128]{1,0:T(8,128)(2,1)}, u32[]{:S(2)}) copy-start(bf16[2048,128]{1,0:T(8,128)(2,1)} %param.12) | copy-start | bytes 1572868
  206.3 5.9 %copy-start.3 = (bf16[2048,128]{1,0:T(8,128)(2,1)S(1)}, bf16[2048,128]{1,0:T(8,128)(2,1)}, u32[]{:S(2)}) copy-start(bf16[2048,128]{1,0:T(8,128)(2,1)} %param.13) | copy-start | bytes 1572868
  249.3 17.9 %all-to-all-start.1 = ((bf16[8,129,128]{2,1,0:T(8,128)(2,1)}), bf16[8,129,128]{2,1,0:T(8,128)(2,1)S(1)}, u32[]{:S(2)}, u32[]{:S(2)}) async-start(bf16[8,129,128]{2,1,0:T(8,128)(2,1)} %broadcast_in_dim.45), calls=%async_computation.1 | async-start | bytes 557056 | tf_op jit(solution)/shard_map/all_to_all | solution.py:12
  271.1 16.5 %all-to-all-start.2 = ((f32[16,1,2048]{2,1,0:T(1,128)}), f32[16,1,2048]{2,1,0:T(1,128)S(1)}, u32[]{:S(2)}, u32[]{:S(2)}) async-start(f32[16,1,2048]{2,1,0:T(1,128)} %broadcast_in_dim.49), calls=%async_computation.2 | async-start | bytes 262144 | tf_op jit(solution)/shard_map/all_to_all | solution.py:12
